TPU v7x, 32 devices: a whole 2x2x4 slice. The times are simulated.
32 devices in a mesh: freq: 4 (over y, x), space: 8 (over z, core).
Axes of the slice: x: 2, y: 2, z: 4, core: 2. Of those that a mesh axis runs over, the one named last changes fastest.
Arguments:
- spectra: bfloat16 [64, 24576, 256], P('freq', 'space'), may hold values from -48 to 48, as said below
- weight: float32 [24576], P('space'), may hold values from 0.25 to 4
- partner: int32 [64], P('freq'), may hold values from 0 to 15
- counts: int32 [64], P('freq'), may hold values from 1 to 8
Outputs:
- modes: bfloat16 [64, 16, 24576], P('freq', None, 'space')
- energy: float32 [64, 8], P('freq')
- coherence: float32 [64, 2, 8, 8], P('freq')
Inputs may be any that keep to these rules, and one draw needn't show every extreme that they name: spectra are finite Fourier coefficients.
All inputs are finite; a program needn't handle non-finite values.
Results may differ from a plain program's by a relative error of at most 0.0045.
Values may be sent and summed in bfloat16 or wider, within the bound.
A program may use at most 128 MiB of HBM per device.

v0:
```python
import jax
import jax.numpy as jnp
from jax import lax
from jax.sharding import PartitionSpec as P

KMAX = 8
ITERS = 4


def from_partner(block, axis, apart):
    count = lax.axis_size(axis)
    route = []
    for low in range(count):
        high = low | 1 << apart
        if high != low and high < count:
            route += [(low, high), (high, low)]
    return lax.ppermute(block, axis, route)


def embed(gram_re, gram_im):
    top = jnp.concatenate([gram_re, -gram_im], axis=2)
    bottom = jnp.concatenate([gram_im, gram_re], axis=2)
    return jnp.concatenate([top, bottom], axis=1)


def apply_operator(operator, basis):
    return jnp.einsum("fkc,fdc->fkd", basis, operator, precision=lax.Precision.HIGHEST)


def orthonormal(vectors, half):
    done = []
    for index in range(vectors.shape[1]):
        vector = vectors[:, index, :]
        for earlier in done:
            early_re, early_im = (earlier[:, :half], earlier[:, half:])
            vec_re, vec_im = (vector[:, :half], vector[:, half:])
            proj_re = jnp.sum(early_re * vec_re + early_im * vec_im, axis=1, keepdims=True)
            proj_im = jnp.sum(early_re * vec_im - early_im * vec_re, axis=1, keepdims=True)
            new_re = vec_re - proj_re * early_re + proj_im * early_im
            new_im = vec_im - proj_re * early_im - proj_im * early_re
            vector = jnp.concatenate([new_re, new_im], axis=1)
        length = jnp.sqrt(jnp.sum(vector * vector, axis=1, keepdims=True) + 1e-06)
        done.append(vector / length)
    return jnp.stack(done, axis=1)


def solve(gram_re, gram_im):
    half = gram_re.shape[1]
    operator = embed(gram_re, gram_im)
    basis = jnp.broadcast_to(
        jnp.eye(KMAX, 2 * half, dtype=jnp.float32), (gram_re.shape[0], KMAX, 2 * half)
    )
    for sweep in range(ITERS):
        basis = orthonormal(apply_operator(operator, basis), half)
    image = apply_operator(operator, basis)
    energy = jnp.sum(basis * image, axis=2)
    return (basis, energy)


def combine(moments, half, total):
    gram_re = (moments[:, :half, :half] + moments[:, half:, half:]) / total
    gram_im = (moments[:, :half, half:] - moments[:, half:, :half]) / total
    return (gram_re, gram_im)


def coefficients(basis, energy, counts):
    half = basis.shape[2] // 2
    ranks = jnp.arange(KMAX, dtype=jnp.int32)[None, :]
    scale = jnp.where(ranks < counts[:, None], 1.0 / jnp.sqrt(energy + 1e-06), 0.0)[:, :, None]
    part_re, part_im = (basis[:, :, :half], basis[:, :, half:])
    upper = jnp.concatenate([part_re, -part_im], axis=2) * scale
    lower = jnp.concatenate([part_im, part_re], axis=2) * scale
    return jnp.concatenate([upper, lower], axis=1).astype(jnp.bfloat16)


def cross_terms(own_modes, other_modes, point_weight, total):
    phi = own_modes.astype(jnp.float32)
    psi = other_modes.astype(jnp.float32)
    wphi = phi * point_weight[None, None, :]
    highest = lax.Precision.HIGHEST

    def inner(left, right):
        return jnp.einsum("fkp,flp->fkl", left, right, precision=highest)

    real_part = inner(wphi[:, :KMAX], psi[:, :KMAX]) + inner(wphi[:, KMAX:], psi[:, KMAX:])
    imag_part = inner(wphi[:, :KMAX], psi[:, KMAX:]) - inner(wphi[:, KMAX:], psi[:, :KMAX])
    return jnp.stack([real_part, imag_part], axis=1) / total


def on_device(spectra, weight, partner, counts):
    groups = spectra.shape[0]
    half = spectra.shape[2] // 2
    total = spectra.shape[1] * lax.axis_size("space")
    weighted = (weight[None, :, None] * spectra).astype(jnp.bfloat16)
    moments = lax.dot_general(
        spectra, weighted, (((1,), (1,)), ((0,), (0,))), preferred_element_type=jnp.float32
    )
    summed = lax.psum(moments, "space")
    gram_re, gram_im = combine(summed, half, total)
    basis, energy = solve(gram_re, gram_im)
    coefficient = coefficients(basis, energy, counts)
    modes = jnp.einsum(
        "fkc,fpc->fkp", coefficient, spectra, preferred_element_type=jnp.float32
    ).astype(jnp.bfloat16)
    levels = lax.axis_size("freq").bit_length() - 1
    mirrored = modes
    for bit in range(levels):
        mirrored = from_partner(mirrored, "freq", bit)
    match = (partner[:, None] == jnp.arange(groups, dtype=jnp.int32)[None, :]).astype(jnp.bfloat16)
    chosen = jnp.einsum("fg,gkp->fkp", match, mirrored, preferred_element_type=jnp.float32).astype(
        jnp.bfloat16
    )
    local = cross_terms(modes, chosen, weight, total)
    coherence = lax.psum(local, "space")
    return (modes, energy, coherence)


def solution(mesh):
    in_specs = (P("freq", "space", None), P("space"), P("freq"), P("freq"))
    out_specs = (P("freq", None, "space"), P("freq", None), P("freq", None, None, None))
    return jax.shard_map(
        on_device, mesh=mesh, in_specs=in_specs, out_specs=out_specs, check_vma=False
    )
```

profile of v0, /device:TPU:0, one launch (start us, length us, event | category | flops | bytes accessed | tf_op | source)
XLA Modules:
  0.0 290.2 jit_solution(2149110146235932898)
XLA Ops:
  7.2 20.7 %fusion.2 = f32[16,256,256]{1,2,0:T(8,128)} fusion(bf16[16,3072,256]{2,1,0:T(8,128)(2,1)} %param.4, f32[3072]{0:T(1024)} %param.5), kind=kOutput, calls=%fused_computation.7 | convolution fusion | flops 6480199680 | bytes 29372416 | tf_op jit(solution)/shard_map/dot_general | solution.py:95
  27.9 99.3 %all-reduce.2.cloned.1.call-done = f32[16,256,256]{1,2,0:T(8,128)} async-done(((f32[16,256,256]{1,2,0:T(8,128)}), f32[16,256,256]{1,2,0:T(8,128)}) %all-reduce.2.cloned.1.call-update) | async-done | bytes 4194320 | tf_op jit(solution)/shard_map/psum | solution.py:98
  127.2 2.8 fusion.80
  130.0 1.9 fusion.42
  132.2 0.1 add_reduce_fusion.111
  132.5 0.1 multiply_reduce_fusion.23
  132.7 0.3 add_reduce_fusion.96
  133.0 0.3 add_reduce_fusion.95
  133.4 0.1 multiply_reduce_fusion.22
  133.6 0.3 add_reduce_fusion.89
  133.8 0.2 add_reduce_fusion.94
  134.4 0.3 add_reduce_fusion.88
  134.6 0.2 add_reduce_fusion.102
  135.1 0.3 add_reduce_fusion.87
  135.4 0.3 add_reduce_fusion.86
  136.0 0.2 add_reduce_fusion.85
  136.5 0.2 add_reduce_fusion.84
  137.4 2.0 fusion.40
  140.2 0.3 add_reduce_fusion.68
  140.5 0.3 add_reduce_fusion.67
  141.1 0.3 add_reduce_fusion.61
  141.4 0.2 add_reduce_fusion.66
  141.9 0.3 add_reduce_fusion.60
  142.2 0.2 add_reduce_fusion.74
  142.7 0.3 add_reduce_fusion.59
  142.9 0.3 add_reduce_fusion.58
  143.5 0.2 add_reduce_fusion.57
  144.0 0.2 add_reduce_fusion.56
  145.0 2.0 fusion.38
  147.8 0.3 add_reduce_fusion.40
  148.1 0.3 add_reduce_fusion.39
  148.6 0.3 add_reduce_fusion.33
  148.9 0.2 add_reduce_fusion.38
  149.4 0.3 add_reduce_fusion.32
  149.7 0.2 add_reduce_fusion.46
  150.2 0.3 add_reduce_fusion.31
  150.5 0.3 add_reduce_fusion.30
  151.0 0.2 add_reduce_fusion.29
  151.6 0.2 add_reduce_fusion.28
  152.5 2.2 fusion.36
  155.5 0.3 add_reduce_fusion.12
  155.8 0.3 add_reduce_fusion.11
  156.4 0.3 add_reduce_fusion.5
  156.7 0.2 add_reduce_fusion.10
  157.2 0.3 add_reduce_fusion.4
  157.5 0.2 add_reduce_fusion.18
  157.9 0.3 add_reduce_fusion.3
  158.2 0.3 add_reduce_fusion.2
  158.8 0.2 add_reduce_fusion.1
  159.3 0.2 add_reduce_fusion
  160.3 2.0 fusion.34
  162.5 12.4 %convert_multiply_fusion = (f32[16,16,3072]{2,1,0:T(8,128)S(1)}, bf16[16,16,3072]{2,1,0:T(8,128)(2,1)}) fusion(f32[3072]{0:T(1024)S(1)} %copy-done, bf16[16,3072,256]{2,1,0:T(8,128)(2,1)} %param.4, bf16[16,16,256]{2,0,1:T(8,128)(2,1)S(1)} %pad_maximum_fusion), kind=kOutput, calls=%fused_computation.6 | convolution fusion | flops 405012480 | bytes 30027776 | tf_op jit(solution)/shard_map/fkc,fpc->fkp/dot_general | solution.py:102
  175.0 1.5 collective-permute-start
  176.5 34.6 %collective-permute-done = bf16[16,16,3072]{2,1,0:T(8,128)(2,1)S(1)} collective-permute-done((bf16[16,16,3072]{2,1,0:T(8,128)(2,1)}, bf16[16,16,3072]{2,1,0:T(8,128)(2,1)S(1)}, u32[]{:S(2)}, u32[]{:S(2)}) %collective-permute-start) | collective-permute-done | bytes 1572896 | tf_op jit(solution)/shard_map/ppermute | solution.py:17
  211.1 1.5 collective-permute-start.1
  212.6 33.6 %collective-permute-done.1 = bf16[16,16,3072]{2,1,0:T(8,128)(2,1)S(1)} collective-permute-done((bf16[16,16,3072]{2,1,0:T(8,128)(2,1)S(1)}, bf16[16,16,3072]{2,1,0:T(8,128)(2,1)S(1)}, u32[]{:S(2)}, u32[]{:S(2)}) %collective-permute-start.1) | collective-permute-done | bytes 1572896 | tf_op jit(solution)/shard_map/ppermute | solution.py:17
  246.1 1.9 convolution_convert_fusion
  248.0 0.1 fusion.82
  248.1 1.8 fusion.6
  249.9 1.8 fusion.4
  251.7 1.5 fusion.15
  253.2 1.8 fusion.21
  255.0 27.5 %psum.15 = f32[16,2,8,8]{3,2,0,1:T(8,128)S(1)} all-reduce(f32[16,2,8,8]{3,2,0,1:T(8,128)S(1)} %maximum_multiply_fusion.2), channel_id=1, replica_groups=mesh['freq'=4,'space'=8] {'space'}, use_global_device_ids=true, to_apply=%region_258.259 | all-reduce | flops 2048 | bytes 16384 | tf_op jit(solution)/shard_map/psum | solution.py:114
  282.6 0.7 copy.52
  (199 shorter events, 11.7 us)
Async XLA Ops:
  7.2 120.1 %all-reduce.2.cloned.1.call-start = ((), (), s32[]{:S(2)}) async-start(), calls=%async_computation | async-start | bytes 8388608 | tf_op jit(solution)/shard_map/psum | solution.py:98
  158.5 3.9 %copy-start.2 = (s32[16]{0:T(128)S(1)}, s32[16]{0:T(128)}, u32[]{:S(2)}) copy-start(s32[16]{0:T(128)} %param.7) | copy-start | bytes 196
  160.0 2.6 copy-start
  162.4 12.6 %copy-start.1 = (f32[16,8]{0,1:T(8,128)}, f32[16,8]{0,1:T(8,128)S(1)}, u32[]{:S(2)}) copy-start(f32[16,8]{0,1:T(8,128)S(1)} %fusion.33) | copy-start | bytes 1540
  162.5 83.6 %copy-start.3 = (s32[16]{0:T(128)S(1)}, s32[16]{0:T(128)}, u32[]{:S(2)}) copy-start(s32[16]{0:T(128)} %param.6) | copy-start | bytes 196
  175.0 36.1 %collective-permute-start = (bf16[16,16,3072]{2,1,0:T(8,128)(2,1)}, bf16[16,16,3072]{2,1,0:T(8,128)(2,1)S(1)}, u32[]{:S(2)}, u32[]{:S(2)}) collective-permute-start(bf16[16,16,3072]{2,1,0:T(8,128)(2,1)} %get-tuple-element.649), channel_id=1, source_target_pairs={{0,8},{8,0},{16,24},{24,16},{1,9},{9,1},{17,25},{25,17},{2,10},{10... | collective-permute-start | bytes 4718600 | tf_op jit(solution)/shard_map/ppermute | solution.py:17
  211.1 35.0 %collective-permute-start.1 = (bf16[16,16,3072]{2,1,0:T(8,128)(2,1)S(1)}, bf16[16,16,3072]{2,1,0:T(8,128)(2,1)S(1)}, u32[]{:S(2)}, u32[]{:S(2)}) collective-permute-start(bf16[16,16,3072]{2,1,0:T(8,128)(2,1)S(1)} %collective-permute-done), channel_id=1, source_target_pairs={{0,16},{16,0},{8,24},{24,8},{1,17},{17,1},{9,25},{25,9},{2,18},{18... | collective-permute-start | bytes 4718600 | tf_op jit(solution)/shard_map/ppermute | solution.py:17
Sparse Core Ops, SparseCore 0:
  28.0 99.1 all-reduce.1
where the time goes:
time: 290 us
  waiting for transfers between devices  168 us (58%)
  matrix products  51.8 us (18%)
  blocking collectives  27.5 us (9%)
  other arithmetic  24.4 us (8%)
  between operations  14.6 us (5%)
  starting transfers between devices  2.98 us (1%)
    psum x1, waiting for transfers between devices, on_device(): summed = lax.psum(moments, 'space')  99.3 us
    ppermute x2, waiting for transfers between devices, from_partner(): return lax.ppermute(block, axis, route)  68.2 us
    psum x1, blocking collectives, on_device(): coherence = lax.psum(local, 'space')  27.5 us
    dot_general x1, matrix products, on_device(): lax.dot_general(spectra, weighted, (((1,), (1,)), ((0,), (0,))), preferre...  20.7 us
    dot_general x1, matrix products, on_device(): jnp.einsum('fkc,fpc->fkp', coefficient, spectra, preferred_element_type=j...  12.4 us
    reduce_sum x44, other arithmetic, orthonormal(): jnp.sum(early_re * vec_re + early_im * vec_im, axis=1, keepdims=True)  10.6 us
    dot_general x5, matrix products, apply_operator(): jnp.einsum('fkc,fdc->fkd', basis, operator, precision=lax.Precision.HIGHEST)  9.94 us
    dot_general x4, matrix products, inner(): return jnp.einsum('fkp,flp->fkl', left, right, precision=highest)  6.86 us
  transfers between devices with their start and end apart: 3, of which 3 were waited for; matrix products, arithmetic and copies ran while one was open for 0% of the time, Pallas kernels for 0%

commit v1 on v0

--- a/solution.py
+++ b/solution.py
@@ -5,6 +5,11 @@
 
 KMAX = 8
 ITERS = 4
+
+
+def summed_here(x, name):
+    parts = lax.all_gather(x, name)
+    return jnp.sum(parts, axis=0)
 
 
 def from_partner(block, axis, apart):
@@ -95,7 +100,7 @@
     moments = lax.dot_general(
         spectra, weighted, (((1,), (1,)), ((0,), (0,))), preferred_element_type=jnp.float32
     )
-    summed = lax.psum(moments, "space")
+    summed = summed_here(moments, "space")
     gram_re, gram_im = combine(summed, half, total)
     basis, energy = solve(gram_re, gram_im)
     coefficient = coefficients(basis, energy, counts)

time: 290 us -> 511 us (1.76)
  waiting for transfers between devices: 168 us -> 361 us
  other arithmetic: 24.4 us -> 38.9 us
  matrix products: 51.8 us -> 59.5 us
  local copies, waits for them, and re-layouts: 1.36 us -> 6.78 us
    all_gather x0 -> x1, waiting for transfers between devices: none -> 291 us  [summed_here(): parts = lax.all_gather(x, name)]
    psum x1 -> x0, waiting for transfers between devices: 99.3 us -> none  [on_device(): summed = lax.psum(moments, 'space')]
    reduce_sum x0 -> x1, other arithmetic: none -> 14.5 us  [summed_here(): return jnp.sum(parts, axis=0)]
    dot_general x5, matrix products: 9.94 us -> 17.8 us  [apply_operator(): jnp.einsum('fkc,fdc->fkd', basis, operator, precision=lax.Precision.HIGHEST)]
    dot_general x0 -> x1, local copies, waits for them, and re-layouts: none -> 5.39 us  [on_device(): lax.dot_general(spectra, weighted, (((1,), (1,)), ((0,), (0,))), preferre...]
where the time goes in v1:
time: 511 us
  waiting for transfers between devices  361 us (71%)
  matrix products  59.5 us (12%)
  other arithmetic  38.9 us (8%)
  blocking collectives  27.3 us (5%)
  between operations  14.6 us (3%)
  local copies, waits for them, and re-layouts  6.78 us (1%)
    all_gather x1, waiting for transfers between devices, summed_here(): parts = lax.all_gather(x, name)  291 us
    ppermute x2, waiting for transfers between devices, from_partner(): return lax.ppermute(block, axis, route)  69.5 us
    psum x1, blocking collectives, on_device(): coherence = lax.psum(local, 'space')  27.3 us
    dot_general x1, matrix products, on_device(): lax.dot_general(spectra, weighted, (((1,), (1,)), ((0,), (0,))), preferre...  20.6 us
    dot_general x5, matrix products, apply_operator(): jnp.einsum('fkc,fdc->fkd', basis, operator, precision=lax.Precision.HIGHEST)  17.8 us
    reduce_sum x1, other arithmetic, summed_here(): return jnp.sum(parts, axis=0)  14.5 us
    dot_general x1, matrix products, on_device(): jnp.einsum('fkc,fpc->fkp', coefficient, spectra, preferred_element_type=j...  12.4 us
    reduce_sum x44, other arithmetic, orthonormal(): jnp.sum(early_re * vec_re + early_im * vec_im, axis=1, keepdims=True)  10.6 us
  transfers between devices with their start and end apart: 3, of which 3 were waited for; matrix products, arithmetic and copies ran while one was open for 0% of the time, Pallas kernels for 0%

profile of v1, /device:TPU:0, one launch (start us, length us, event | category | flops | bytes accessed | tf_op | source)
XLA Modules:
  0.0 511.1 jit_solution(1717100442794676299)
XLA Ops:
  7.2 20.6 %fusion.2 = f32[16,256,256]{1,2,0:T(8,128)} fusion(bf16[16,3072,256]{2,1,0:T(8,128)(2,1)} %param.4, f32[3072]{0:T(1024)} %param.5), kind=kOutput, calls=%fused_computation.7 | convolution fusion | flops 6480199680 | bytes 29372416 | tf_op jit(solution)/shard_map/dot_general | solution.py:100
  27.8 5.4 %copy.49 = f32[16,256,256]{2,1,0:T(8,128)} copy(f32[16,256,256]{1,2,0:T(8,128)} %fusion.2) | data formatting | bytes 8388608 | tf_op jit(solution)/shard_map/dot_general | solution.py:100
  33.3 291.5 %all-gather.3.cloned.1.call-done = f32[128,256,256]{2,1,0:T(8,128)} async-done(((f32[16,256,256]{2,1,0:T(8,128)}), f32[128,256,256]{2,1,0:T(8,128)}) %all-gather.3.cloned.1.call-update) | async-done | bytes 33554448 | tf_op jit(solution)/shard_map/all_gather | solution.py:11
  324.7 14.5 %reduce_sum.2322 = f32[16,256,256]{2,1,0:T(8,128)} reduce(f32[8,16,256,256]{3,2,1,0:T(8,128)} %bitcast.166, f32[]{:T(128)} %constant.3.clone.1), dimensions={0}, to_apply=%region_0.0 | reduce | flops 7340032 | bytes 37748740 | tf_op jit(solution)/shard_map/reduce_sum | solution.py:12
  339.3 2.8 fusion.80
  342.0 3.4 fusion.42
  345.9 0.1 add_reduce_fusion.111
  346.3 0.3 add_reduce_fusion.96
  346.6 0.3 add_reduce_fusion.95
  347.2 0.3 add_reduce_fusion.89
  347.5 0.2 add_reduce_fusion.94
  348.0 0.3 add_reduce_fusion.88
  348.3 0.2 add_reduce_fusion.102
  348.7 0.3 add_reduce_fusion.87
  349.0 0.3 add_reduce_fusion.86
  349.6 0.2 add_reduce_fusion.85
  350.1 0.2 add_reduce_fusion.84
  351.0 3.5 fusion.40
  355.4 0.3 add_reduce_fusion.68
  355.7 0.3 add_reduce_fusion.67
  356.3 0.3 add_reduce_fusion.61
  356.6 0.2 add_reduce_fusion.66
  357.1 0.3 add_reduce_fusion.60
  357.4 0.2 add_reduce_fusion.74
  357.8 0.3 add_reduce_fusion.59
  358.1 0.3 add_reduce_fusion.58
  358.7 0.2 add_reduce_fusion.57
  359.2 0.2 add_reduce_fusion.56
  360.1 3.7 fusion.38
  364.7 0.3 add_reduce_fusion.40
  365.0 0.3 add_reduce_fusion.39
  365.6 0.3 add_reduce_fusion.33
  365.9 0.2 add_reduce_fusion.38
  366.4 0.3 add_reduce_fusion.32
  366.7 0.2 add_reduce_fusion.46
  367.1 0.3 add_reduce_fusion.31
  367.4 0.3 add_reduce_fusion.30
  368.0 0.2 add_reduce_fusion.29
  368.5 0.2 add_reduce_fusion.28
  369.4 3.5 fusion.36
  373.8 0.3 add_reduce_fusion.12
  374.1 0.3 add_reduce_fusion.11
  374.7 0.3 add_reduce_fusion.5
  375.0 0.2 add_reduce_fusion.10
  375.5 0.3 add_reduce_fusion.4
  375.8 0.2 add_reduce_fusion.18
  376.2 0.3 add_reduce_fusion.3
  376.5 0.3 add_reduce_fusion.2
  377.1 0.2 add_reduce_fusion.1
  377.6 0.2 add_reduce_fusion
  378.6 3.5 fusion.34
  382.4 12.4 %convert_multiply_fusion = (f32[16,16,3072]{2,1,0:T(8,128)S(1)}, bf16[16,16,3072]{2,1,0:T(8,128)(2,1)}) fusion(f32[3072]{0:T(1024)S(1)} %copy-done, bf16[16,3072,256]{2,1,0:T(8,128)(2,1)} %param.4, bf16[16,16,256]{2,0,1:T(8,128)(2,1)S(1)} %pad_maximum_fusion), kind=kOutput, calls=%fused_computation.6 | convolution fusion | flops 405012480 | bytes 30027776 | tf_op jit(solution)/shard_map/fkc,fpc->fkp/dot_general | solution.py:107
  394.9 1.5 collective-permute-start
  396.3 35.3 %collective-permute-done = bf16[16,16,3072]{2,1,0:T(8,128)(2,1)S(1)} collective-permute-done((bf16[16,16,3072]{2,1,0:T(8,128)(2,1)}, bf16[16,16,3072]{2,1,0:T(8,128)(2,1)S(1)}, u32[]{:S(2)}, u32[]{:S(2)}) %collective-permute-start) | collective-permute-done | bytes 1572896 | tf_op jit(solution)/shard_map/ppermute | solution.py:22
  431.6 1.5 collective-permute-start.1
  433.1 34.2 %collective-permute-done.1 = bf16[16,16,3072]{2,1,0:T(8,128)(2,1)S(1)} collective-permute-done((bf16[16,16,3072]{2,1,0:T(8,128)(2,1)S(1)}, bf16[16,16,3072]{2,1,0:T(8,128)(2,1)S(1)}, u32[]{:S(2)}, u32[]{:S(2)}) %collective-permute-start.1) | collective-permute-done | bytes 1572896 | tf_op jit(solution)/shard_map/ppermute | solution.py:22
  467.3 1.9 convolution_convert_fusion
  469.2 0.1 fusion.82
  469.3 1.8 fusion.6
  471.1 1.8 fusion.4
  472.9 1.5 fusion.15
  474.4 1.8 fusion.21
  476.2 27.3 %psum.7 = f32[16,2,8,8]{3,2,0,1:T(8,128)S(1)} all-reduce(f32[16,2,8,8]{3,2,0,1:T(8,128)S(1)} %maximum_multiply_fusion.2), channel_id=1, replica_groups=mesh['freq'=4,'space'=8] {'space'}, use_global_device_ids=true, to_apply=%region_258.259 | all-reduce | flops 2048 | bytes 16384 | tf_op jit(solution)/shard_map/psum | solution.py:119
  503.5 0.7 copy.94
  (201 shorter events, 12.0 us)
Async XLA Ops:
  7.2 317.6 %all-gather.3.cloned.1.call-start = ((), (), s32[]{:S(2)}) async-start(), calls=%async_computation | async-start | bytes 37748736 | tf_op jit(solution)/shard_map/all_gather | solution.py:11
  376.8 5.4 %copy-start.2 = (s32[16]{0:T(128)S(1)}, s32[16]{0:T(128)}, u32[]{:S(2)}) copy-start(s32[16]{0:T(128)} %param.7) | copy-start | bytes 196
  378.3 4.1 copy-start
  382.2 12.6 %copy-start.1 = (f32[16,8]{0,1:T(8,128)}, f32[16,8]{0,1:T(8,128)S(1)}, u32[]{:S(2)}) copy-start(f32[16,8]{0,1:T(8,128)S(1)} %fusion.33) | copy-start | bytes 1540
  382.4 84.9 %copy-start.3 = (s32[16]{0:T(128)S(1)}, s32[16]{0:T(128)}, u32[]{:S(2)}) copy-start(s32[16]{0:T(128)} %param.6) | copy-start | bytes 196
  394.9 36.8 %collective-permute-start = (bf16[16,16,3072]{2,1,0:T(8,128)(2,1)}, bf16[16,16,3072]{2,1,0:T(8,128)(2,1)S(1)}, u32[]{:S(2)}, u32[]{:S(2)}) collective-permute-start(bf16[16,16,3072]{2,1,0:T(8,128)(2,1)} %get-tuple-element.652), channel_id=1, source_target_pairs={{0,8},{8,0},{16,24},{24,16},{1,9},{9,1},{17,25},{25,17},{2,10},{10... | collective-permute-start | bytes 4718600 | tf_op jit(solution)/shard_map/ppermute | solution.py:22
  431.6 35.7 %collective-permute-start.1 = (bf16[16,16,3072]{2,1,0:T(8,128)(2,1)S(1)}, bf16[16,16,3072]{2,1,0:T(8,128)(2,1)S(1)}, u32[]{:S(2)}, u32[]{:S(2)}) collective-permute-start(bf16[16,16,3072]{2,1,0:T(8,128)(2,1)S(1)} %collective-permute-done), channel_id=1, source_target_pairs={{0,16},{16,0},{8,24},{24,8},{1,17},{17,1},{9,25},{25,9},{2,18},{18... | collective-permute-start | bytes 4718600 | tf_op jit(solution)/shard_map/ppermute | solution.py:22
Sparse Core Ops, SparseCore 0:
  33.4 291.3 all-gather.2
